TPU v7x, 512 devices: a whole 4x4x16 slice. The times are simulated.
512 devices in a mesh: dp: 64 (over z_lo, x, core), ens: 8 (over y, z_hi).
Axes of the slice: x: 4, y: 4, z: 16 (z_hi: 2, z_lo: 8; z = z_hi * 8 + z_lo), core: 2. Of those that a mesh axis runs over, the one named last changes fastest.
Arguments:
- embeddings: bfloat16 [49152, 1024], P('dp'), may hold values from -6 to 6
- valid_mask: int32 [49152], P('dp'), may hold values 0 or 1
- first_weight: bfloat16 [8, 1024, 4096], P(None, 'dp', 'ens'), may hold values from -0.1875 to 0.1875
- second_weight: bfloat16 [8, 4096, 128], P(None, 'ens'), may hold values from -0.09375 to 0.09375
- thresholds: int32 [8], replicated, may hold values from -256 to 256
Outputs:
- mean_logits: float32 [49152, 128], P('dp')
- kept_share: float32 [8], P('ens')
- agree_share: float32 [8], P('ens')
All inputs are finite; a program needn't handle non-finite values. No bound on the sum of `valid_mask` on one device may be relied on, other than what follows from the above.
Results may differ from a plain program's by a relative error of at most 0.0044.
Values may be sent and summed in bfloat16 or wider, within the bound.
A program may use at most 64 MiB of HBM per device.

v0:
```python
import functools

import jax
import jax.numpy as jnp
from jax import lax
from jax.experimental import pallas as pl
from jax.experimental.pallas import tpu as pltpu
from jax.sharding import PartitionSpec as P

MESH = pl.DeviceIdType.MESH
COLS = 512
LAG = 2
PARTS = 2
SLOTS = 2


def geometry(mesh):
    line = [tuple(d.coords) for d in mesh.devices.reshape(mesh.devices.shape[0], -1)[:, 0]]
    cores = sum(c == line[0] for c in line)
    chips = line[::cores]
    inner = 1
    if len(chips) > 1:
        axis = [a != b for a, b in zip(chips[0], chips[1])].index(True)
        while inner < len(chips) and chips[inner][axis] == chips[0][axis] + inner:
            inner += 1
    return len(chips) // inner, inner, cores


def turned_period(nz, nx):
    even = (nz - 1) * nx - (nx - 1)
    slope = (nz - 1) * (nx - 1) + (nz - 1) * (nx - 1)
    share = 1.0 - even / slope if slope else 0.0
    return round(1 / share) if share > 0 else 0


def kernel(
    geo, n_ens, emb_hbm, mask_ref, fw_hbm, sw_hbm, thr_ref, out_ref, kept_ref, agree_ref,
    w, emb, sw, acc, part, sc, tot,
    local_sem, emb_sem, send_sem, recv_sem, part_send, part_recv, sc_send, sc_recv, tot_sem, core_send, core_recv,
):
    nz, nx, nc = geo
    n_dp = nz * nx * nc
    n_chips = nz * nx
    members, rows, units = fw_hbm.shape
    per_member = units // COLS
    chunks = members * per_member
    docs, classes = out_ref.shape
    period = turned_period(nz, nx)
    reach = nz - 1 + nx - 1
    slots = send_sem.shape[0]

    me = lax.axis_index("dp")
    ens = lax.axis_index("ens")
    core = lax.rem(me, nc)
    chip = me // nc
    z, x = chip // nx, lax.rem(chip, nx)

    def origin_rows(origin):
        return pl.ds(pl.multiple_of(origin * rows, rows), rows)

    def own_copy(c):
        cols = pl.ds(pl.multiple_of(lax.rem(c, per_member) * COLS, COLS), COLS)
        return pltpu.make_async_copy(
            fw_hbm.at[c // per_member, :, cols], w.at[c, origin_rows(me), :], local_sem.at[c]
        )

    for c in range(chunks):
        own_copy(jnp.int32(c)).start()
    emb_copy = pltpu.make_async_copy(emb_hbm, emb, emb_sem.at[0])
    sw_copy = pltpu.make_async_copy(sw_hbm, sw, emb_sem.at[1])
    emb_copy.start()
    sw_copy.start()

    barrier = pltpu.get_barrier_semaphore()
    dirs = []
    if nz > 1:
        dirs += [("z", 1), ("z", -1)]
    if nx > 1:
        dirs += [("x", 1), ("x", -1)]
    dirs += [("c", k) for k in range(1, nc)]

    def target(d):
        kind, k = d
        if kind == "z":
            return me + k * nx * nc
        if kind == "x":
            return me + k * nc
        return chip * nc + lax.rem(core + k, nc)

    def there(d):
        kind, k = d
        if kind == "c":
            return None
        at, n = (z, nz) if kind == "z" else (x, nx)
        return at + 1 < n if k > 0 else at > 0

    waits = jnp.int32(nc - 1 + n_ens - 1)
    for d in dirs:
        ok = there(d)
        if ok is None:
            pl.semaphore_signal(barrier, inc=1, device_id={"dp": target(d)}, device_id_type=MESH)
        else:
            @pl.when(ok)
            def _():
                pl.semaphore_signal(barrier, inc=1, device_id={"dp": target(d)}, device_id_type=MESH)
            waits = waits + ok.astype(jnp.int32)
    for k in range(1, n_ens):
        pl.semaphore_signal(
            barrier, inc=1, device_id={"ens": lax.rem(ens + k, n_ens)}, device_id_type=MESH
        )
    pl.semaphore_wait(barrier, waits)

    def turned(c):
        if not period:
            return jnp.bool_(False)
        return lax.rem(c * nc + core, period) == period // 2

    def goes(d, c, zo, xo):
        kind, k = d
        if kind == "c":
            return c >= 0
        inner_first = turned(c)
        if kind == "z":
            away = (z >= zo) if k > 0 else (z <= zo)
            return away & there(d) & ((xo == x) | inner_first)
        away = (x >= xo) if k > 0 else (x <= xo)
        return away & there(d) & ((zo == z) | jnp.logical_not(inner_first))

    def sending(i, d, c, zo, xo):
        place = zo * nx + xo
        origin = place * nc + core
        block = w.at[c, origin_rows(origin), :]
        if d[0] == "c":
            sems = core_send.at[c, d[1]], core_recv.at[c, d[1]]
        else:
            sems = send_sem.at[lax.rem(c, slots), i, place], recv_sem.at[c, place]
        return pltpu.make_async_remote_copy(
            src_ref=block, dst_ref=block, send_sem=sems[0], recv_sem=sems[1],
            device_id={"dp": target(d)}, device_id_type=MESH,
        )

    def from_cores(c, k):
        blocks = w.at[c, pl.ds(0, n_chips * rows), :]
        return pltpu.make_async_remote_copy(
            src_ref=blocks, dst_ref=blocks,
            send_sem=core_send.at[c, k], recv_sem=core_recv.at[c, k],
            device_id={"dp": target(("c", k))}, device_id_type=MESH,
        )

    def arrived(c, place):
        block = w.at[c, origin_rows(place * nc + core), :]
        pltpu.make_async_remote_copy(
            src_ref=block, dst_ref=block, send_sem=send_sem.at[0, 0, 0], recv_sem=recv_sem.at[c, place],
            device_id={"dp": target(dirs[-1])}, device_id_type=MESH,
        ).wait_recv()

    def place_of(k):
        kz, kx = divmod(k, nx)
        return lax.rem(z + kz, nz), lax.rem(x + kx, nx)

    acc[...] = jnp.zeros_like(acc)

    def compute(done):
        @pl.when(done >= 0)
        def _():
            @pl.when(done == 0)
            def _():
                emb_copy.wait()
                sw_copy.wait()
            for o in range(1, nc):
                from_cores(done, o).wait_recv()
            m = done // per_member
            cols = pl.ds(pl.multiple_of(lax.rem(done, per_member) * COLS, COLS), COLS)
            hidden = jnp.maximum(
                jnp.dot(emb[...], w[done], preferred_element_type=jnp.float32), 0.0
            ).astype(jnp.bfloat16)
            acc[m] += jnp.dot(hidden, sw[m, cols, :], preferred_element_type=jnp.float32)

    def step(t, carry):
        for k in range(n_chips):
            zo, xo = place_of(k)
            c = t - LAG * (jnp.abs(z - zo) + jnp.abs(x - xo))

            @pl.when((c >= 0) & (c < chunks))
            def _():
                if k == 0:
                    own_copy(c).wait()
                else:
                    arrived(c, zo * nx + xo)
                for i, d in enumerate(dirs):
                    if d[0] == "c":
                        sending(i, d, c, zo, xo).start()
                        continue

                    @pl.when((c >= slots) & goes(d, c - slots, zo, xo))
                    def _():
                        sending(i, d, c - slots, zo, xo).wait_send()

                    @pl.when(goes(d, c, zo, xo))
                    def _():
                        sending(i, d, c, zo, xo).start()

            if k == n_chips - 1:
                compute(t - LAG * reach - 1)
        return carry

    lax.fori_loop(0, chunks + LAG * reach + 1, step, 0)

    lines = sc.shape[1]
    levels = lax.broadcasted_iota(jnp.int32, (lines, classes), 1).astype(jnp.float32)
    grades = (2.0 * levels / (classes - 1) - 1.0) * jnp.sqrt(jnp.float32(3.0 / classes))
    line = lax.broadcasted_iota(jnp.int32, (lines, classes), 0)
    own_scores = jnp.zeros((lines, docs), jnp.float32)
    for m in range(members):
        own_scores += lax.dot_general(
            jnp.where(line == m, grades, 0.0), acc[m], (((1,), (1,)), ((), ())),
            precision=lax.Precision.HIGHEST, preferred_element_type=jnp.float32,
        )
    sc[ens] = own_scores

    def sc_copy(k):
        return pltpu.make_async_remote_copy(
            src_ref=sc.at[ens], dst_ref=sc.at[ens], send_sem=sc_send.at[k], recv_sem=sc_recv.at[ens],
            device_id={"ens": lax.rem(ens + k, n_ens)}, device_id_type=MESH,
        )

    def part_copy(k, b):
        piece = part.at[ens, pl.ds(b * (docs // PARTS), docs // PARTS), :]
        return pltpu.make_async_remote_copy(
            src_ref=piece, dst_ref=piece, send_sem=part_send.at[k, b], recv_sem=part_recv.at[ens, b],
            device_id={"ens": lax.rem(ens + k, n_ens)}, device_id_type=MESH,
        )

    for k in range(1, n_ens):
        sc_copy(k).start()
    for b in range(PARTS):
        piece = pl.ds(b * (docs // PARTS), docs // PARTS)
        total = acc[0, piece, :]
        for m in range(1, members):
            total += acc[m, piece, :]
        part[ens, piece, :] = (total * (1.0 / members)).astype(jnp.bfloat16)
        for k in range(1, n_ens):
            part_copy(k, b).start()

    for k in range(1, n_ens):
        other = lax.rem(ens + k, n_ens)
        pltpu.make_async_remote_copy(
            src_ref=sc.at[other], dst_ref=sc.at[other], send_sem=sc_send.at[k], recv_sem=sc_recv.at[other],
            device_id={"ens": other}, device_id_type=MESH,
        ).wait_recv()
    scores = sc[0]
    for k in range(1, n_ens):
        scores += sc[k]
    row = lax.broadcasted_iota(jnp.int32, (lines, docs), 0)
    cutoff = jnp.zeros((lines, docs), jnp.float32)
    mean_cutoff = jnp.float32(0.0)
    for m in range(members):
        level = thr_ref[m].astype(jnp.float32) * (1.0 / 256.0)
        cutoff = jnp.where(row == m, level, cutoff)
        mean_cutoff += level * (1.0 / members)
    kept = mask_ref[...].reshape(1, docs).astype(jnp.float32) * jax.nn.sigmoid(4.0 * (scores - cutoff))
    ens_score = jnp.sum(scores, axis=0, keepdims=True) * (1.0 / members)
    ens_kept = jax.nn.sigmoid(4.0 * (ens_score - mean_cutoff))
    kept_sum = jnp.sum(kept, axis=1, keepdims=True)
    agree_sum = jnp.sum(kept * ens_kept, axis=1, keepdims=True)
    lane = lax.broadcasted_iota(jnp.int32, (lines, 128), 1)
    tot[me] = jnp.where(lane == 0, kept_sum, jnp.where(lane == 1, agree_sum, 0.0))

    def tot_copy(k):
        return pltpu.make_async_remote_copy(
            src_ref=tot.at[me], dst_ref=tot.at[me], send_sem=tot_sem.at[0], recv_sem=tot_sem.at[1],
            device_id={"dp": lax.rem(me + k, n_dp)}, device_id_type=MESH,
        )

    tiles = tot.at[pl.ds(0, n_dp - 1)]
    all_tot = pltpu.make_async_remote_copy(
        src_ref=tiles, dst_ref=tiles, send_sem=tot_sem.at[0], recv_sem=tot_sem.at[1],
        device_id={"dp": lax.rem(me + 1, n_dp)}, device_id_type=MESH,
    )

    for k in range(1, n_dp):
        tot_copy(k).start()

    for b in range(PARTS):
        piece = pl.ds(b * (docs // PARTS), docs // PARTS)
        for k in range(1, n_ens):
            other = lax.rem(ens + k, n_ens)
            block = part.at[other, piece, :]
            pltpu.make_async_remote_copy(
                src_ref=block, dst_ref=block, send_sem=part_send.at[k, b], recv_sem=part_recv.at[other, b],
                device_id={"ens": other}, device_id_type=MESH,
            ).wait_recv()
        total = part[0, piece, :].astype(jnp.float32)
        for k in range(1, n_ens):
            total += part[k, piece, :].astype(jnp.float32)
        out_ref[piece, :] = total

    all_tot.wait_recv()
    sums = tot[0]
    for k in range(1, n_dp):
        sums += tot[k]
    sums = sums / docs
    own = members // n_ens
    row = lax.broadcasted_iota(jnp.int32, (lines, 128), 0)
    for j in range(own):
        mine = row == ens * own + j
        kept_ref[j] = jnp.sum(jnp.where(mine & (lane == 0), sums, 0.0))
        agree_ref[j] = jnp.sum(jnp.where(mine & (lane == 1), sums, 0.0))

    for k in range(n_chips):
        zo, xo = place_of(k)
        for c in range(max(0, chunks - slots), chunks):
            for i, d in enumerate(dirs):
                if d[0] != "c":
                    @pl.when(goes(d, jnp.int32(c), zo, xo))
                    def _():
                        sending(i, d, jnp.int32(c), zo, xo).wait_send()
    for c in range(chunks):
        for k in range(1, nc):
            from_cores(c, k).wait_send()
    for k in range(1, n_ens):
        sc_copy(k).wait_send()
        for b in range(PARTS):
            part_copy(k, b).wait_send()
    all_tot.wait_send()


def solution(mesh):
    geo = geometry(mesh)
    nz, nx, nc = geo
    n_dp, n_ens = mesh.shape["dp"], mesh.shape["ens"]

    def on_device(embeddings, valid_mask, first_weight, second_weight, thresholds):
        docs, width = embeddings.shape
        members, rows, units = first_weight.shape
        classes = second_weight.shape[2]
        chunks = members * units // COLS
        own = members // n_ens
        lines = -(-members // 8) * 8
        dma = pltpu.SemaphoreType.DMA
        hbm, vmem, smem = (pl.BlockSpec(memory_space=s) for s in (pl.ANY, pltpu.VMEM, pltpu.SMEM))
        return pl.pallas_call(
            functools.partial(kernel, geo, n_ens),
            out_shape=(
                jax.ShapeDtypeStruct((docs, classes), jnp.float32),
                jax.ShapeDtypeStruct((own,), jnp.float32),
                jax.ShapeDtypeStruct((own,), jnp.float32),
            ),
            in_specs=[hbm, vmem, hbm, hbm, smem],
            out_specs=(vmem, smem, smem),
            scratch_shapes=[
                pltpu.VMEM((chunks, width, COLS), jnp.bfloat16),
                pltpu.VMEM((docs, width), jnp.bfloat16),
                pltpu.VMEM(second_weight.shape, jnp.bfloat16),
                pltpu.VMEM((members, docs, classes), jnp.float32),
                pltpu.VMEM((n_ens, docs, classes), jnp.bfloat16),
                pltpu.VMEM((n_ens, lines, docs), jnp.float32),
                pltpu.VMEM((n_dp, lines, 128), jnp.float32),
                dma((chunks,)),
                dma((2,)),
                dma((SLOTS, 4, nz * nx)),
                dma((chunks, nz * nx)),
                dma((n_ens, PARTS)),
                dma((n_ens, PARTS)),
                dma((n_ens,)),
                dma((n_ens,)),
                dma((2,)),
                dma((chunks, nc)),
                dma((chunks, nc)),
            ],
            compiler_params=pltpu.CompilerParams(
                collective_id=0, has_side_effects=True, vmem_limit_bytes=63 * 1024 * 1024
            ),
        )(embeddings, valid_mask, first_weight, second_weight, thresholds)

    return jax.shard_map(
        on_device,
        mesh=mesh,
        in_specs=(P("dp", None), P("dp"), P(None, "dp", "ens"), P(None, "ens", None), P()),
        out_specs=(P("dp", None), P("ens"), P("ens")),
        check_vma=False,
    )
```

profile of v0, /device:TPU:1, one launch (start us, length us, event | category | flops | bytes accessed | tf_op | source)
XLA Modules:
  0.0 175.8 jit_solution(10364338337698780311)
XLA Ops:
  0.6 169.8 %shard_map.76 = (f32[768,128]{1,0:T(8,128)}, f32[1]{0:T(128)}, f32[1]{0:T(128)}) custom-call(bf16[768,1024]{1,0:T(8,128)(2,1)} %emb_hbm.1, s32[768]{0:T(1024)} %mask_ref.1, bf16[8,16,512]{2,1,0:T(8,128)(2,1)} %fw_hbm.1, bf16[8,512,128]{2,1,0:T(8,128)(2,1)} %sw_hbm.1, s32[8]{0:T(128)} %thr_ref.1), custom_call_target="tpu_custom_call" | custom-call | tf_op jit(solution)/shard_map/pallas_call | solution.py:342
  170.4 1.8 %copy.11 = f32[768,128]{1,0:T(8,128)} copy(f32[768,128]{1,0:T(8,128)} %get-tuple-element.6) | data formatting | bytes 786432
where the time goes:
time: 176 us
  Pallas kernels  170 us (97%)
  between operations  4.21 us (2%)
  local copies, waits for them, and re-layouts  1.77 us (1%)
    pallas_call x1, Pallas kernels, on_device(): pl.pallas_call(functools.partial(kernel, geo, n_ens), out_shape=(jax.Shap...  170 us

commit v1 on v0

v1 whole, which is shorter than its diff:
```python
import functools

import jax
import jax.numpy as jnp
from jax import lax
from jax.experimental import pallas as pl
from jax.experimental.pallas import tpu as pltpu
from jax.sharding import PartitionSpec as P

MESH = pl.DeviceIdType.MESH
NZ, NX, NC, NY, NH = 8, 4, 2, 4, 2
CHUNKS = 4
DELTA = 2


def kernel(
    emb_hbm, mask_ref, fw_hbm, sw_hbm, thr_ref, out_ref, kept_ref, agree_ref,
    w, emb, bmat, acc, part_s, part_r, sc_s, sc_r, zp_s, zp_r, zc_s, zc_r, fin, mask4, tot1, tot2,
    in_sem, z_recv, x_recv, d_recv, z_send, x_send, d_send, y_send, y_recv, h_send, h_recv, t_send, t_recv,
):
    members, _, rows, units = fw_hbm.shape[0], 0, fw_hbm.shape[1], fw_hbm.shape[2]
    docs, classes = out_ref.shape
    share = docs // NY
    per = members // CHUNKS
    me = lax.axis_index("dp")
    ens = lax.axis_index("ens")
    core = lax.rem(me, NC)
    x = lax.rem(me // NC, NX)
    z = me // (NC * NX)
    y = ens // NH
    zh = lax.rem(ens, NH)

    def dp_of(z_, x_, c_):
        return (z_ * NX + x_) * NC + c_

    x_up, x_dn, x_far = lax.rem(x + 1, NX), lax.rem(x + NX - 1, NX), lax.rem(x + 2, NX)
    sib = {"dp": dp_of(z, x, 1 - core)}
    to_xu = {"dp": dp_of(z, x_up, core)}
    to_xd = {"dp": dp_of(z, x_dn, core)}
    to_zu = {"dp": dp_of(z + 1, x, core)}
    to_zd = {"dp": dp_of(z - 1, x, core)}
    has_zu, has_zd = z + 1 < NZ, z > 0

    own_in = pltpu.make_async_copy(fw_hbm, w.at[:, z, x * NC + core], in_sem.at[0])
    emb_in = pltpu.make_async_copy(emb_hbm, emb, in_sem.at[1])
    sw_in = pltpu.make_async_copy(sw_hbm, bmat.at[:, :, pl.ds(0, classes)], in_sem.at[2])
    own_in.start()
    sw_in.start()
    emb_in.start()

    barrier = pltpu.get_barrier_semaphore()
    for d in (to_xu, to_xd, sib):
        pl.semaphore_signal(barrier, inc=1, device_id=d, device_id_type=MESH)
    for k in range(1, NY * NH):
        pl.semaphore_signal(
            barrier, inc=1, device_id={"ens": lax.rem(ens + k, NY * NH)}, device_id_type=MESH
        )
    for ok, d in ((has_zu, to_zu), (has_zd, to_zd)):
        @pl.when(ok)
        def _():
            pl.semaphore_signal(barrier, inc=1, device_id=d, device_id_type=MESH)
    pl.semaphore_wait(
        barrier, jnp.int32(3 + NY * NH - 1) + has_zu.astype(jnp.int32) + has_zd.astype(jnp.int32)
    )

    acc[...] = jnp.zeros_like(acc)

    def piece(h, zo, xo):
        return w.at[pl.ds(h * per, per), zo, xo * NC + core]

    def rcopy(ref, send, recv, to):
        return pltpu.make_async_remote_copy(
            src_ref=ref, dst_ref=ref, send_sem=send, recv_sem=recv, device_id=to, device_id_type=MESH
        )

    def to_sibling(h, zo, xo):
        rcopy(piece(h, zo, xo), d_send.at[0], d_recv.at[h], sib).start()

    def x_out(h, zo):
        rcopy(piece(h, zo, x), x_send.at[0], x_recv.at[h, zo, 0], to_xu).start()
        rcopy(piece(h, zo, x), x_send.at[1], x_recv.at[h, zo, 1], to_xd).start()
        to_sibling(h, zo, x)

    def z_out(h, zo, s, up):
        if up:
            rcopy(piece(h, zo, x), z_send.at[0, s], z_recv.at[h, zo], to_zu).start()
        else:
            rcopy(piece(h, zo, x), z_send.at[1, s], z_recv.at[h, zo], to_zd).start()

    def plus_way(h, zo):
        flip = (zo > z).astype(jnp.int32)
        return lax.rem(zo + flip + h, 2) == 0

    def z_event(h, s):
        @pl.when(s == 0)
        def _():
            @pl.when(has_zu)
            def _():
                z_out(h, z, s, True)

            @pl.when(has_zd)
            def _():
                z_out(h, z, s, False)
            x_out(h, z)

        for up in (True, False):
            zo = z - s if up else z + s

            @pl.when((s > 0) & (zo >= 0) & (zo < NZ))
            def _():
                rcopy(piece(h, zo, x), z_send.at[0, 0], z_recv.at[h, zo], to_xu).wait_recv()

                @pl.when(has_zu if up else has_zd)
                def _():
                    z_out(h, zo, s, up)
                x_out(h, zo)

    def both_ways(s, act):
        @pl.when((s >= 0) & (s < NZ) & (z - s >= 0))
        def _():
            act(z - s)

        @pl.when((s > 0) & (s < NZ) & (z + s < NZ))
        def _():
            act(z + s)

    def x_event(h, s):
        def act(zo):
            plus = plus_way(h, zo)
            rcopy(piece(h, zo, x_dn), x_send.at[2], x_recv.at[h, zo, 0], to_xu).wait_recv()

            @pl.when(plus)
            def _():
                rcopy(piece(h, zo, x_dn), x_send.at[2], x_recv.at[h, zo, 2], to_xu).start()
            to_sibling(h, zo, x_dn)
            rcopy(piece(h, zo, x_up), x_send.at[2], x_recv.at[h, zo, 1], to_xu).wait_recv()

            @pl.when(jnp.logical_not(plus))
            def _():
                rcopy(piece(h, zo, x_up), x_send.at[2], x_recv.at[h, zo, 2], to_xd).start()
            to_sibling(h, zo, x_up)
        both_ways(s, act)

    def far_event(h, s):
        def act(zo):
            rcopy(piece(h, zo, x_far), x_send.at[2], x_recv.at[h, zo, 2], to_xu).wait_recv()
            to_sibling(h, zo, x_far)
        both_ways(s, act)

    level = lax.broadcasted_iota(jnp.int32, (units, classes), 1)
    grade = (2.0 * level.astype(jnp.float32) / (classes - 1) - 1.0) * jnp.sqrt(jnp.float32(3.0 / classes))

    def grade_column(m):
        column = jnp.sum(bmat[m, :, 0:classes].astype(jnp.float32) * grade, axis=1, keepdims=True)
        high = column.astype(jnp.bfloat16).astype(jnp.float32)
        mid = (column - high).astype(jnp.bfloat16).astype(jnp.float32)
        low = column - high - mid
        both = jnp.where(level == m, high, jnp.where(level == members + m, mid, jnp.where(level == 2 * members + m, low, 0.0)))
        bmat[m, :, classes:2 * classes] = both.astype(jnp.bfloat16)

    def compute(m):
        if CHUNKS == members:
            arrived = True
        else:
            arrived = lax.rem(m, per) == 0

        @pl.when(arrived)
        def _():
            h = m // per
            size = w.at[pl.ds(0, per), :, pl.ds(0, NX)]
            rcopy(size, d_send.at[0], d_recv.at[h], sib).wait_recv()
        hidden = jnp.maximum(
            jnp.dot(emb[...], w[m].reshape(NZ * NX * NC * rows, units), preferred_element_type=jnp.float32), 0.0
        ).astype(jnp.bfloat16)
        acc[...] += jnp.dot(hidden, bmat[m], preferred_element_type=jnp.float32)

    lag = NZ + 2

    def slot(t, carry):
        @pl.when(t == 0)
        def _():
            own_in.wait()
        for h in range(CHUNKS):
            s = t - DELTA * h

            @pl.when((s >= 0) & (s < NZ))
            def _():
                z_event(h, s)
        for h in range(CHUNKS):
            x_event(h, t - DELTA * h - 1)
        for h in range(CHUNKS):
            far_event(h, t - DELTA * h - 2)

        @pl.when(t == 0)
        def _():
            sw_in.wait()
            emb_in.wait()

        @pl.when(t < members)
        def _():
            grade_column(t)

        @pl.when(t >= lag)
        def _():
            compute(t - lag)
        return carry

    lax.fori_loop(0, lag + members, slot, 0)

    for j in range(NY):
        rows_j = jnp.concatenate(
            [acc[j * share:(j + 1) * share, classes:2 * classes], jnp.zeros((256 - share, classes), jnp.float32)], axis=0
        )
        turned = rows_j.T
        sc_s[j] = turned[0:8] + turned[8:16] + turned[16:24]

    def y_dev(k):
        return {"ens": lax.rem(y + k, NY) * NH + zh}

    def sc_copy(k):
        return pltpu.make_async_remote_copy(
            src_ref=sc_s.at[lax.rem(y + k, NY)], dst_ref=sc_r.at[y], send_sem=y_send.at[0, k], recv_sem=y_recv.at[0, y],
            device_id=y_dev(k), device_id_type=MESH,
        )

    def part_copy(k):
        return pltpu.make_async_remote_copy(
            src_ref=part_s.at[lax.rem(y + k, NY)], dst_ref=part_r.at[y], send_sem=y_send.at[1, k], recv_sem=y_recv.at[1, y],
            device_id=y_dev(k), device_id_type=MESH,
        )

    def fin_copy(k):
        return pltpu.make_async_remote_copy(
            src_ref=fin.at[y], dst_ref=fin.at[y], send_sem=y_send.at[2, k], recv_sem=y_recv.at[2, y],
            device_id=y_dev(k), device_id_type=MESH,
        )

    def y_wait(i, buf, k):
        other = lax.rem(y + k, NY)
        rcopy(buf.at[other], y_send.at[i, k], y_recv.at[i, other], y_dev(k)).wait_recv()

    for k in range(1, NY):
        sc_copy(k).start()
    for j in range(NY):
        part_s[j] = (acc[j * share:(j + 1) * share, 0:classes] * (1.0 / members)).astype(jnp.bfloat16)
    for k in range(1, NY):
        part_copy(k).start()

    z_dev = {"ens": y * NH + (1 - zh)}
    zc_copy = pltpu.make_async_remote_copy(
        src_ref=zc_s, dst_ref=zc_r, send_sem=h_send.at[0], recv_sem=h_recv.at[0], device_id=z_dev, device_id_type=MESH
    )
    zp_copy = pltpu.make_async_remote_copy(
        src_ref=zp_s, dst_ref=zp_r, send_sem=h_send.at[1], recv_sem=h_recv.at[1], device_id=z_dev, device_id_type=MESH
    )
    scores = sc_s[y]
    for k in range(1, NY):
        y_wait(0, sc_r, k)
        scores += sc_r[lax.rem(y + k, NY)]
    zc_s[...] = scores
    zc_copy.start()
    means = acc[pl.ds(pl.multiple_of(y * share, share), share), 0:classes] * (1.0 / members)
    for k in range(1, NY):
        y_wait(1, part_r, k)
        means += part_r[lax.rem(y + k, NY)].astype(jnp.float32)
    zp_s[...] = means.astype(jnp.bfloat16)
    zp_copy.start()

    mask_row = jnp.broadcast_to(mask_ref[...].reshape(1, docs).astype(jnp.float32), (8, docs))
    lane2 = lax.broadcasted_iota(jnp.int32, (8, 256), 1)
    for j in range(NY):
        moved = mask_row if j == 0 else pltpu.roll(mask_row, docs - j * share, 1)
        mask4[j] = jnp.where(lane2 < share, moved[:, 0:256], 0.0)
    row2 = lax.broadcasted_iota(jnp.int32, (8, 256), 0)
    cutoff = jnp.zeros((8, 256), jnp.float32)
    mean_cutoff = jnp.float32(0.0)
    for m in range(members):
        cut = thr_ref[m].astype(jnp.float32) * (1.0 / 256.0)
        cutoff = jnp.where(row2 == m, cut, cutoff)
        mean_cutoff += cut * (1.0 / members)
    zc_copy.wait_recv()
    scores = zc_s[...] + zc_r[...]
    kept = mask4[y] * jax.nn.sigmoid(4.0 * (scores - cutoff))
    ens_score = jnp.sum(scores, axis=0, keepdims=True) * (1.0 / members)
    ens_kept = jax.nn.sigmoid(4.0 * (ens_score - mean_cutoff))
    kept_sum = jnp.sum(kept, axis=1, keepdims=True)
    agree_sum = jnp.sum(kept * ens_kept, axis=1, keepdims=True)
    lane = lax.broadcasted_iota(jnp.int32, (8, 128), 1)
    row = lax.broadcasted_iota(jnp.int32, (8, 128), 0)
    line = jnp.sum(
        jnp.where(lane == row, kept_sum, 0.0) + jnp.where(lane == row + 8, agree_sum, 0.0), axis=0, keepdims=True
    )
    first = y * NC + core
    tot1[first, 0:1, :] = line

    def tot1_copy(k):
        to = lax.rem(first + k, NY * NC)
        return pltpu.make_async_remote_copy(
            src_ref=tot1.at[first, pl.ds(0, 1)], dst_ref=tot1.at[first, pl.ds(0, 1)],
            send_sem=t_send.at[0], recv_sem=t_recv.at[0],
            device_id={"dp": dp_of(z, x, lax.rem(to, NC)), "ens": (to // NC) * NH + zh}, device_id_type=MESH,
        )

    for k in range(1, NY * NC):
        tot1_copy(k).start()
    peers = NY * NC - 1
    all1 = rcopy(tot1.at[pl.ds(0, peers), pl.ds(0, 1)], t_send.at[0], t_recv.at[0], sib)
    all1.wait_recv()
    line = tot1[0, 0:1, :]
    for k in range(1, NY * NC):
        line += tot1[k, 0:1, :]
    second = x * NZ + z
    tot2[second, 0:1, :] = line
    deep = zh * NZ + z
    for dx in range(NX):
        for dz in range(-NZ // 2, NZ // 2):
            if dx == 0 and dz == 0:
                continue
            zz = lax.rem(deep + dz + NZ * NH, NZ * NH)
            pltpu.make_async_remote_copy(
                src_ref=tot2.at[second, pl.ds(0, 1)], dst_ref=tot2.at[second, pl.ds(0, 1)],
                send_sem=t_send.at[1], recv_sem=t_recv.at[1],
                device_id={"dp": dp_of(lax.rem(zz, NZ), lax.rem(x + dx, NX), core), "ens": y * NH + zz // NZ},
                device_id_type=MESH,
            ).start()

    zp_copy.wait_recv()
    fin[y] = (zp_s[...].astype(jnp.float32) + zp_r[...].astype(jnp.float32)).astype(jnp.bfloat16)
    for k in range(1, NY):
        fin_copy(k).start()

    column = w.at[:, :, 0]
    rcopy(column, x_send.at[0], d_recv.at[0], sib).wait_send()
    rcopy(column, x_send.at[1], d_recv.at[0], sib).wait_send()
    rcopy(column, x_send.at[2], d_recv.at[0], sib).wait_send()
    rcopy(w.at[:, :, pl.ds(0, NX)], d_send.at[0], d_recv.at[0], sib).wait_send()
    block = w.at[:, 0, 0]
    for s in range(NZ - 1):
        @pl.when(has_zu & (z - s >= 0))
        def _():
            rcopy(block, z_send.at[0, s], d_recv.at[0], sib).wait_send()

        @pl.when(has_zd & (z + s < NZ))
        def _():
            rcopy(block, z_send.at[1, s], d_recv.at[0], sib).wait_send()
    for k in range(1, NY):
        sc_copy(k).wait_send()
        part_copy(k).wait_send()
    zc_copy.wait_send()
    zp_copy.wait_send()
    all1.wait_send()

    out_ref[pl.ds(pl.multiple_of(y * share, share), share), :] = fin[y].astype(jnp.float32)
    for k in range(1, NY):
        y_wait(2, fin, k)
        other = lax.rem(y + k, NY)
        out_ref[pl.ds(pl.multiple_of(other * share, share), share), :] = fin[other].astype(jnp.float32)
    for k in range(1, NY):
        fin_copy(k).wait_send()

    all2 = rcopy(tot2.at[pl.ds(0, NX * NZ - 1), pl.ds(0, 1)], t_send.at[1], t_recv.at[1], sib)
    all2.wait_recv()
    line = tot2[0, 0:1, :]
    for k in range(1, NX * NZ):
        line += tot2[k, 0:1, :]
    line = line * (1.0 / docs)
    at = lax.broadcasted_iota(jnp.int32, (1, 128), 1)
    kept_ref[0] = jnp.sum(jnp.where(at == ens, line, 0.0))
    agree_ref[0] = jnp.sum(jnp.where(at == ens + 8, line, 0.0))
    all2.wait_send()


def solution(mesh):
    def on_device(embeddings, valid_mask, first_weight, second_weight, thresholds):
        docs, width = embeddings.shape
        members, rows, units = first_weight.shape
        classes = second_weight.shape[2]
        share = docs // NY
        dma = pltpu.SemaphoreType.DMA
        bf16, f32 = jnp.bfloat16, jnp.float32
        hbm, vmem, smem = (pl.BlockSpec(memory_space=s) for s in (pl.ANY, pltpu.VMEM, pltpu.SMEM))
        return pl.pallas_call(
            kernel,
            out_shape=(
                jax.ShapeDtypeStruct((docs, classes), f32),
                jax.ShapeDtypeStruct((1,), f32),
                jax.ShapeDtypeStruct((1,), f32),
            ),
            in_specs=[hbm, vmem, hbm, hbm, smem],
            out_specs=(vmem, smem, smem),
            scratch_shapes=[
                pltpu.VMEM((members, NZ, NX * NC, rows, units), bf16),
                pltpu.VMEM((docs, width), bf16),
                pltpu.VMEM((members, units, 2 * classes), bf16),
                pltpu.VMEM((docs, 2 * classes), f32),
                pltpu.VMEM((NY, share, classes), bf16),
                pltpu.VMEM((NY, share, classes), bf16),
                pltpu.VMEM((NY, 8, 256), f32),
                pltpu.VMEM((NY, 8, 256), f32),
                pltpu.VMEM((share, classes), bf16),
                pltpu.VMEM((share, classes), bf16),
                pltpu.VMEM((8, 256), f32),
                pltpu.VMEM((8, 256), f32),
                pltpu.VMEM((NY, share, classes), bf16),
                pltpu.VMEM((NY, 8, 256), f32),
                pltpu.VMEM((NY * NC, 8, 128), f32),
                pltpu.VMEM((NX * NZ, 8, 128), f32),
                dma((3,)),
                dma((CHUNKS, NZ)),
                dma((CHUNKS, NZ, 3)),
                dma((CHUNKS,)),
                dma((2, NZ)),
                dma((3,)),
                dma((1,)),
                dma((3, NY)),
                dma((3, NY)),
                dma((2,)),
                dma((2,)),
                dma((2,)),
                dma((2,)),
            ],
            compiler_params=pltpu.CompilerParams(
                collective_id=0, has_side_effects=True, vmem_limit_bytes=63 * 1024 * 1024
            ),
        )(embeddings, valid_mask, first_weight, second_weight, thresholds)

    return jax.shard_map(
        on_device,
        mesh=mesh,
        in_specs=(P("dp", None), P("dp"), P(None, "dp", "ens"), P(None, "ens", None), P()),
        out_specs=(P("dp", None), P("ens"), P("ens")),
        check_vma=False,
    )
```

time: 176 us -> 104 us (0.59)
  Pallas kernels: 170 us -> 97.8 us
    pallas_call x1, Pallas kernels: 170 us -> 97.8 us  [on_device(): pl.pallas_call(kernel, out_shape=(jax.ShapeDtypeStruct((docs, classes), f...]
where the time goes in v1:
time: 104 us
  Pallas kernels  97.8 us (94%)
  between operations  4.21 us (4%)
  local copies, waits for them, and re-layouts  1.77 us (2%)
    pallas_call x1, Pallas kernels, on_device(): pl.pallas_call(kernel, out_shape=(jax.ShapeDtypeStruct((docs, classes), f...  97.8 us

profile of v1, /device:TPU:1, one launch (start us, length us, event | category | flops | bytes accessed | tf_op | source)
XLA Modules:
  0.0 103.8 jit_solution(3649243215054425997)
XLA Ops:
  0.6 97.8 %shard_map.76 = (f32[768,128]{1,0:T(8,128)}, f32[1]{0:T(128)}, f32[1]{0:T(128)}) custom-call(bf16[768,1024]{1,0:T(8,128)(2,1)} %emb_hbm.1, s32[768]{0:T(1024)} %mask_ref.1, bf16[8,16,512]{2,1,0:T(8,128)(2,1)} %fw_hbm.1, bf16[8,512,128]{2,1,0:T(8,128)(2,1)} %sw_hbm.1, s32[8]{0:T(128)} %thr_ref.1), custom_call_target="tpu_custom_call" | custom-call | tf_op jit(solution)/shard_map/pallas_call | solution.py:382
  98.4 1.8 %copy.11 = f32[768,128]{1,0:T(8,128)} copy(f32[768,128]{1,0:T(8,128)} %get-tuple-element.6) | data formatting | bytes 786432
